TPU v7x, 32 devices: a whole 2x2x4 slice. The times are simulated.
32 devices in a mesh: dp: 8 (over z, y), sy: 2 (over x), sx: 2 (over core).
Axes of the slice: x: 2, y: 2, z: 4, core: 2. Of those that a mesh axis runs over, the one named last changes fastest.
Arguments:
- features: bfloat16 [8, 56, 56, 256], P('dp', 'sy', 'sx'), may hold values from -8 to 8
- labels: int32 [8], P('dp'), may hold values from 0 to 999
- grid: int32 [2], replicated, may hold values from 0 to 49
- w_reduce: bfloat16 [3, 256, 64], P(None, None, 'dp'), may hold values from -0.375 to 0.375
- w_spatial: bfloat16 [3, 3, 3, 64, 64], P(None, None, None, None, 'dp'), may hold values from -0.25 to 0.25
- w_expand: bfloat16 [3, 64, 256], P(None, None, 'dp'), may hold values from -0.75 to 0.75
- w_class: bfloat16 [256, 1000], P('dp'), may hold values from -1.5 to 1.5
- dir_reduce: bfloat16 [2, 3, 256, 64], P(None, None, None, 'dp'), may hold values from -6 to 6
- dir_spatial: bfloat16 [2, 3, 3, 3, 64, 64], P(None, None, None, None, None, 'dp'), may hold values from -6 to 6
- dir_expand: bfloat16 [2, 3, 64, 256], P(None, None, None, 'dp'), may hold values from -6 to 6
- dir_class: bfloat16 [2, 256, 1000], P(None, 'dp'), may hold values from -6 to 6
- gain_mid: float32 [3, 2, 64], replicated, may hold values from 0.5 to 1.5
- shift_mid: float32 [3, 2, 64], replicated, may hold values from -3 to 3
- gain_out: float32 [3, 256], replicated, may hold values from 0.5 to 1.5
- shift_out: float32 [3, 256], replicated, may hold values from -3 to 3
Outputs:
- section_out: bfloat16 [8, 56, 56, 256], P('dp', 'sy', 'sx')
- image_loss: float32 [8], P('dp')
- mean_loss: float32 [], replicated
All inputs are finite; a program needn't handle non-finite values.
Results may differ from a plain program's by a relative error of at most 0.012.
Values may be sent and summed in bfloat16 or wider, within the bound.
A program may use at most 64 MiB of HBM per device.

v0:
```python
import jax
import jax.numpy as jnp
from jax import lax
from jax.sharding import PartitionSpec as P

BLOCKS = 3
GRID = 50
EPS_NORM = 1e-06
EPS_BN = 1e-05


def extended(cells, sides, width):
    for axis, dim in sides:
        count = lax.axis_size(axis)
        ends = count - 1
        head = lax.slice_in_dim(cells, 0, width, axis=dim)
        tail = lax.slice_in_dim(cells, cells.shape[dim] - width, cells.shape[dim], axis=dim)
        cells = jnp.concatenate(
            [
                lax.ppermute(tail, axis, [(i, (i + 1) % count) for i in range(ends)]),
                cells,
                lax.ppermute(head, axis, [((i + 1) % count, i) for i in range(ends)]),
            ],
            axis=dim,
        )
    return cells


def coefficients(grid):
    values = grid.astype(jnp.float32)
    alpha = (2.0 * values + 1.0 - GRID) / GRID
    return (alpha[0], alpha[1])


def filter_ratio(base, direction):
    base_norm = jnp.sqrt(jnp.sum(jnp.square(base.astype(jnp.float32)), axis=0, keepdims=True))
    dir_norm = jnp.sqrt(
        jnp.sum(jnp.square(direction.astype(jnp.float32)), axis=0, keepdims=True) + EPS_NORM
    )
    return base_norm / dir_norm


def combine_filters(base, dir_a, dir_b, alpha_a, alpha_b):
    ratio_a = filter_ratio(base, dir_a)
    ratio_b = filter_ratio(base, dir_b)
    value = (
        base.astype(jnp.float32)
        + alpha_a * ratio_a * dir_a.astype(jnp.float32)
        + alpha_b * ratio_b * dir_b.astype(jnp.float32)
    )
    return value.astype(jnp.bfloat16)


def perturbed_product(left, base, dir_a, dir_b, alpha_a, alpha_b):
    local = combine_filters(base, dir_a, dir_b, alpha_a, alpha_b)
    return jnp.dot(
        left, lax.all_gather(local, "dp", axis=1, tiled=True), preferred_element_type=jnp.float32
    )


def normalize(y, gain, shift, count):
    mean = lax.psum(jnp.sum(y, axis=0), ("dp", "sy", "sx")) / count
    centred = y - mean
    var = lax.psum(jnp.sum(centred * centred, axis=0), ("dp", "sy", "sx")) / count
    return centred * lax.rsqrt(var + EPS_BN) * gain + shift


def padded_tile(inner):
    return extended(inner, (("sy", 1), ("sx", 2)), 1)


def per_device(
    features,
    labels,
    grid,
    w_reduce,
    w_spatial,
    w_expand,
    w_class,
    dir_reduce,
    dir_spatial,
    dir_expand,
    dir_class,
    gain_mid,
    shift_mid,
    gain_out,
    shift_out,
):
    alpha_a, alpha_b = coefficients(grid)
    images, rows, cols, width = features.shape
    tiles = lax.axis_size("sy") * lax.axis_size("sx")
    count = images * rows * cols * lax.axis_size("dp") * tiles
    inner_width = w_spatial.shape[3]
    current = features
    for block in range(BLOCKS):
        flat = current.reshape(-1, width)
        first = perturbed_product(
            flat, w_reduce[block], dir_reduce[0, block], dir_reduce[1, block], alpha_a, alpha_b
        )
        first = jax.nn.relu(
            normalize(first, gain_mid[block, 0], shift_mid[block, 0], count)
        ).astype(jnp.bfloat16)
        framed = padded_tile(first.reshape(images, rows, cols, inner_width))
        patches = jnp.concatenate(
            [framed[:, i : i + rows, j : j + cols, :] for i in range(3) for j in range(3)], axis=-1
        )
        patches = patches.reshape(-1, 9 * inner_width)
        spatial_base = w_spatial[block].reshape(9 * inner_width, -1)
        spatial_a = dir_spatial[0, block].reshape(9 * inner_width, -1)
        spatial_b = dir_spatial[1, block].reshape(9 * inner_width, -1)
        second = perturbed_product(patches, spatial_base, spatial_a, spatial_b, alpha_a, alpha_b)
        second = jax.nn.relu(
            normalize(second, gain_mid[block, 1], shift_mid[block, 1], count)
        ).astype(jnp.bfloat16)
        third = perturbed_product(
            second, w_expand[block], dir_expand[0, block], dir_expand[1, block], alpha_a, alpha_b
        )
        third = normalize(third, gain_out[block], shift_out[block], count)
        current = (
            jax.nn.relu(flat.astype(jnp.float32) + third)
            .astype(jnp.bfloat16)
            .reshape(images, rows, cols, width)
        )
    pooled_part = jnp.sum(current.astype(jnp.float32), axis=(1, 2))
    pooled = (lax.psum(pooled_part, ("sy", "sx")) / (rows * cols * tiles)).astype(jnp.bfloat16)
    class_a = dir_class[0]
    class_b = dir_class[1]
    norm_base, norm_a, norm_b = lax.psum(
        (
            jnp.sum(jnp.square(w_class.astype(jnp.float32)), axis=0),
            jnp.sum(jnp.square(class_a.astype(jnp.float32)), axis=0),
            jnp.sum(jnp.square(class_b.astype(jnp.float32)), axis=0),
        ),
        "dp",
    )
    ratio_a = jnp.sqrt(norm_base) / jnp.sqrt(norm_a + EPS_NORM)
    ratio_b = jnp.sqrt(norm_base) / jnp.sqrt(norm_b + EPS_NORM)
    local_class = (
        w_class.astype(jnp.float32)
        + alpha_a * ratio_a * class_a.astype(jnp.float32)
        + alpha_b * ratio_b * class_b.astype(jnp.float32)
    ).astype(jnp.bfloat16)
    logits = jnp.dot(
        pooled,
        lax.all_gather(local_class, "dp", axis=0, tiled=True),
        preferred_element_type=jnp.float32,
    )
    summed = jnp.log(jnp.sum(jnp.exp(logits), axis=1))
    classes = lax.broadcasted_iota(jnp.int32, logits.shape, 1)
    picked = jnp.sum(jnp.where(classes == labels[:, None], logits, 0.0), axis=1)
    image_loss = summed - picked
    mean_loss = lax.psum(jnp.sum(image_loss), "dp") / (images * lax.axis_size("dp"))
    return (current, image_loss, mean_loss)


def solution(mesh):
    in_specs = (
        P("dp", "sy", "sx", None),
        P("dp"),
        P(),
        P(None, None, "dp"),
        P(None, None, None, None, "dp"),
        P(None, None, "dp"),
        P("dp", None),
        P(None, None, None, "dp"),
        P(None, None, None, None, None, "dp"),
        P(None, None, None, "dp"),
        P(None, "dp", None),
        P(),
        P(),
        P(),
        P(),
    )
    out_specs = (P("dp", "sy", "sx", None), P("dp"), P())
    return jax.shard_map(
        per_device, mesh=mesh, in_specs=in_specs, out_specs=out_specs, check_vma=False
    )
```

profile of v0, /device:TPU:0, one launch (start us, length us, event | category | flops | bytes accessed | tf_op | source)
XLA Modules:
  0.0 1203.1 jit_solution(10325314932056759414)
XLA Ops:
  1.9 1.0 fusion.64
  2.8 1.0 multiply_reduce_fusion.10
  4.7 1.3 multiply_multiply_fusion.5
  6.1 1.3 multiply_multiply_fusion.11
  7.4 1.3 multiply_multiply_fusion.17
  8.8 32.4 %all_gather.30 = bf16[256,64]{0,1:T(8,128)(2,1)S(1)} all-gather(bf16[256,8]{0,1:T(8,128)(2,1)S(1)} %get-tuple-element.100), channel_id=1, replica_groups=mesh['dp'=8,'sy'=2,'sx'=2] {'dp'}, dimensions={1}, use_global_device_ids=true | all-gather | bytes 36864 | tf_op jit(solution)/shard_map/all_gather | solution.py:57
  41.2 1.1 reshape.399
  42.7 39.6 %psum.161 = f32[64]{0:T(128)S(1)} all-reduce(f32[64]{0:T(128)S(1)} %get-tuple-element.142), channel_id=1, replica_groups=mesh['dp'=8,'sy'=2,'sx'=2] {'dp','sy','sx'}, use_global_device_ids=true, to_apply=%region_4.0 | all-reduce | flops 64 | bytes 512 | tf_op jit(solution)/shard_map/psum | solution.py:62
  82.4 40.7 %psum.162 = f32[64]{0:T(128)S(1)} all-reduce(f32[64]{0:T(128)S(1)} %multiply_reduce_fusion.8), channel_id=1, replica_groups=mesh['dp'=8,'sy'=2,'sx'=2] {'dp','sy','sx'}, use_global_device_ids=true, to_apply=%region_6.0 | all-reduce | flops 64 | bytes 512 | tf_op jit(solution)/shard_map/psum | solution.py:64
  124.7 4.2 collective-permute-start
  128.8 1.3 collective-permute-start.1
  130.6 32.7 %all_gather.31 = bf16[576,64]{0,1:T(8,128)(2,1)} all-gather(bf16[576,8]{0,1:T(8,128)(2,1)S(1)} %add_convert_fusion.2), channel_id=1, replica_groups=mesh['dp'=8,'sy'=2,'sx'=2] {'dp'}, dimensions={1}, use_global_device_ids=true | all-gather | bytes 82944 | tf_op jit(solution)/shard_map/all_gather | solution.py:57
  166.4 32.6 %all_gather.34 = bf16[576,64]{0,1:T(8,128)(2,1)} all-gather(bf16[576,8]{0,1:T(8,128)(2,1)S(1)} %add_convert_fusion.1), channel_id=1, replica_groups=mesh['dp'=8,'sy'=2,'sx'=2] {'dp'}, dimensions={1}, use_global_device_ids=true | all-gather | bytes 82944 | tf_op jit(solution)/shard_map/all_gather | solution.py:57
  200.1 36.1 %all-reduce = (f32[1000]{0:T(1024)S(1)}, f32[1000]{0:T(1024)S(1)}, f32[1000]{0:T(1024)S(1)}) all-reduce(f32[1000]{0:T(1024)S(1)} %get-tuple-element.4, f32[1000]{0:T(1024)S(1)} %get-tuple-element.174, f32[1000]{0:T(1024)S(1)} %get-tuple-element.3), channel_id=1, replica_groups=mesh['dp'=8,'sy'=2,'sx'=2] {'dp'}, use_global_device_ids=true, to_apply=%region_70.71 | all-reduce | flops 3000 | bytes 24000 | tf_op jit(solution)/shard_map/psum | solution.py:128
  236.2 1.3 multiply_multiply_fusion.1
  237.6 31.2 %all_gather.39 = bf16[256,1000]{1,0:T(8,128)(2,1)S(1)} all-gather(bf16[32,1000]{1,0:T(8,128)(2,1)S(1)} %fusion.14), channel_id=1, replica_groups=mesh['dp'=8,'sy'=2,'sx'=2] {'dp'}, dimensions={0}, use_global_device_ids=true | all-gather | bytes 576000 | tf_op jit(solution)/shard_map/all_gather | solution.py:145
  268.8 1.3 multiply_multiply_fusion.15
  270.2 1.3 multiply_multiply_fusion.3
  272.2 32.5 %all_gather.32 = bf16[64,256]{0,1:T(8,128)(2,1)} all-gather(bf16[64,32]{0,1:T(8,128)(2,1)S(1)} %get-tuple-element.95), channel_id=1, replica_groups=mesh['dp'=8,'sy'=2,'sx'=2] {'dp'}, dimensions={1}, use_global_device_ids=true | all-gather | bytes 36864 | tf_op jit(solution)/shard_map/all_gather | solution.py:57
  304.9 1.3 collective-permute-start.2
  306.2 1.3 collective-permute-start.3
  307.5 32.1 %all_gather.33 = bf16[256,64]{0,1:T(8,128)(2,1)} all-gather(bf16[256,8]{0,1:T(8,128)(2,1)S(1)} %get-tuple-element.101), channel_id=1, replica_groups=mesh['dp'=8,'sy'=2,'sx'=2] {'dp'}, dimensions={1}, use_global_device_ids=true | all-gather | bytes 36864 | tf_op jit(solution)/shard_map/all_gather | solution.py:57
  343.7 0.9 copy-done.6
  346.1 0.9 copy-done.1
  347.1 0.9 copy-done.11
  348.3 37.4 %psum.163 = f32[64]{0:T(128)S(1)} all-reduce(f32[64]{0:T(128)S(1)} %get-tuple-element.144), channel_id=1, replica_groups=mesh['dp'=8,'sy'=2,'sx'=2] {'dp','sy','sx'}, use_global_device_ids=true, to_apply=%region_11.12 | all-reduce | flops 64 | bytes 512 | tf_op jit(solution)/shard_map/psum | solution.py:62
  386.0 42.8 %psum.164 = f32[64]{0:T(128)S(1)} all-reduce(f32[64]{0:T(128)S(1)} %multiply_reduce_fusion.7), channel_id=1, replica_groups=mesh['dp'=8,'sy'=2,'sx'=2] {'dp','sy','sx'}, use_global_device_ids=true, to_apply=%region_13.14 | all-reduce | flops 64 | bytes 512 | tf_op jit(solution)/shard_map/psum | solution.py:64
  429.9 38.1 %psum.165 = f32[256]{0:T(256)S(1)} all-reduce(f32[256]{0:T(256)S(1)} %get-tuple-element.146), channel_id=1, replica_groups=mesh['dp'=8,'sy'=2,'sx'=2] {'dp','sy','sx'}, use_global_device_ids=true, to_apply=%region_18.19 | all-reduce | flops 256 | bytes 2048 | tf_op jit(solution)/shard_map/psum | solution.py:62
  468.1 41.9 %psum.166 = f32[256]{0:T(256)S(1)} all-reduce(f32[256]{0:T(256)S(1)} %multiply_reduce_fusion.2), channel_id=1, replica_groups=mesh['dp'=8,'sy'=2,'sx'=2] {'dp','sy','sx'}, use_global_device_ids=true, to_apply=%region_20.21 | all-reduce | flops 256 | bytes 2048 | tf_op jit(solution)/shard_map/psum | solution.py:64
  511.8 38.3 %psum.167 = f32[64]{0:T(128)S(1)} all-reduce(f32[64]{0:T(128)S(1)} %get-tuple-element.148), channel_id=1, replica_groups=mesh['dp'=8,'sy'=2,'sx'=2] {'dp','sy','sx'}, use_global_device_ids=true, to_apply=%region_25.26 | all-reduce | flops 64 | bytes 512 | tf_op jit(solution)/shard_map/psum | solution.py:62
  550.2 41.9 %psum.168 = f32[64]{0:T(128)S(1)} all-reduce(f32[64]{0:T(128)S(1)} %multiply_reduce_fusion.6), channel_id=1, replica_groups=mesh['dp'=8,'sy'=2,'sx'=2] {'dp','sy','sx'}, use_global_device_ids=true, to_apply=%region_27.28 | all-reduce | flops 64 | bytes 512 | tf_op jit(solution)/shard_map/psum | solution.py:64
  593.1 4.2 collective-permute-start.4
  597.3 32.5 %all_gather.35 = bf16[64,256]{0,1:T(8,128)(2,1)} all-gather(bf16[64,32]{0,1:T(8,128)(2,1)S(1)} %copy-done.24), channel_id=1, replica_groups=mesh['dp'=8,'sy'=2,'sx'=2] {'dp'}, dimensions={1}, use_global_device_ids=true | all-gather | bytes 36864 | tf_op jit(solution)/shard_map/all_gather | solution.py:57
  629.9 1.3 collective-permute-start.5
  631.2 4.2 collective-permute-done.5
  635.6 1.3 collective-permute-start.6
  636.9 1.3 collective-permute-start.7
  638.2 30.6 %all_gather.36 = bf16[256,64]{0,1:T(8,128)(2,1)S(1)} all-gather(bf16[256,8]{0,1:T(8,128)(2,1)S(1)} %get-tuple-element.99), channel_id=1, replica_groups=mesh['dp'=8,'sy'=2,'sx'=2] {'dp'}, dimensions={1}, use_global_device_ids=true | all-gather | bytes 36864 | tf_op jit(solution)/shard_map/all_gather | solution.py:57
  671.1 0.9 constant_dynamic-update-slice_fusion.23
  672.7 1.7 copy.33
  675.4 0.9 copy-done.7
  677.9 0.9 copy-done.10
  679.1 36.9 %psum.169 = f32[64]{0:T(128)S(1)} all-reduce(f32[64]{0:T(128)S(1)} %get-tuple-element.150), channel_id=1, replica_groups=mesh['dp'=8,'sy'=2,'sx'=2] {'dp','sy','sx'}, use_global_device_ids=true, to_apply=%region_32.33 | all-reduce | flops 64 | bytes 512 | tf_op jit(solution)/shard_map/psum | solution.py:62
  716.2 41.0 %psum.170 = f32[64]{0:T(128)S(1)} all-reduce(f32[64]{0:T(128)S(1)} %multiply_reduce_fusion.5), channel_id=1, replica_groups=mesh['dp'=8,'sy'=2,'sx'=2] {'dp','sy','sx'}, use_global_device_ids=true, to_apply=%region_34.35 | all-reduce | flops 64 | bytes 512 | tf_op jit(solution)/shard_map/psum | solution.py:64
  758.3 39.7 %psum.171 = f32[256]{0:T(256)S(1)} all-reduce(f32[256]{0:T(256)S(1)} %get-tuple-element.152), channel_id=1, replica_groups=mesh['dp'=8,'sy'=2,'sx'=2] {'dp','sy','sx'}, use_global_device_ids=true, to_apply=%region_39.40 | all-reduce | flops 256 | bytes 2048 | tf_op jit(solution)/shard_map/psum | solution.py:62
  798.1 40.3 %psum.172 = f32[256]{0:T(256)S(1)} all-reduce(f32[256]{0:T(256)S(1)} %multiply_reduce_fusion.1), channel_id=1, replica_groups=mesh['dp'=8,'sy'=2,'sx'=2] {'dp','sy','sx'}, use_global_device_ids=true, to_apply=%region_41.42 | all-reduce | flops 256 | bytes 2048 | tf_op jit(solution)/shard_map/psum | solution.py:64
  839.7 39.7 %psum.173 = f32[64]{0:T(128)S(1)} all-reduce(f32[64]{0:T(128)S(1)} %get-tuple-element.154), channel_id=1, replica_groups=mesh['dp'=8,'sy'=2,'sx'=2] {'dp','sy','sx'}, use_global_device_ids=true, to_apply=%region_46.47 | all-reduce | flops 64 | bytes 512 | tf_op jit(solution)/shard_map/psum | solution.py:62
  879.5 40.3 %psum.174 = f32[64]{0:T(128)S(1)} all-reduce(f32[64]{0:T(128)S(1)} %multiply_reduce_fusion.4), channel_id=1, replica_groups=mesh['dp'=8,'sy'=2,'sx'=2] {'dp','sy','sx'}, use_global_device_ids=true, to_apply=%region_48.49 | all-reduce | flops 64 | bytes 512 | tf_op jit(solution)/shard_map/psum | solution.py:64
  920.9 4.2 collective-permute-start.8
  925.1 32.5 %all_gather.37 = bf16[576,64]{0,1:T(8,128)(2,1)} all-gather(bf16[576,8]{0,1:T(8,128)(2,1)S(1)} %add_convert_fusion), channel_id=1, replica_groups=mesh['dp'=8,'sy'=2,'sx'=2] {'dp'}, dimensions={1}, use_global_device_ids=true | all-gather | bytes 82944 | tf_op jit(solution)/shard_map/all_gather | solution.py:57
  957.6 1.3 collective-permute-start.9
  959.0 4.2 collective-permute-done.9
  963.4 1.3 collective-permute-start.10
  964.7 1.3 collective-permute-start.11
  966.0 32.8 %all_gather.38 = bf16[64,256]{0,1:T(8,128)(2,1)} all-gather(bf16[64,32]{0,1:T(8,128)(2,1)S(1)} %copy-done.23), channel_id=1, replica_groups=mesh['dp'=8,'sy'=2,'sx'=2] {'dp'}, dimensions={1}, use_global_device_ids=true | all-gather | bytes 36864 | tf_op jit(solution)/shard_map/all_gather | solution.py:57
  1003.5 0.9 copy-done.8
  1006.0 0.9 copy-done.2
  1006.9 0.9 copy-done.12
  1008.1 36.9 %psum.175 = f32[64]{0:T(128)S(1)} all-reduce(f32[64]{0:T(128)S(1)} %get-tuple-element.156), channel_id=1, replica_groups=mesh['dp'=8,'sy'=2,'sx'=2] {'dp','sy','sx'}, use_global_device_ids=true, to_apply=%region_53.54 | all-reduce | flops 64 | bytes 512 | tf_op jit(solution)/shard_map/psum | solution.py:62
  1045.2 41.8 %psum.176 = f32[64]{0:T(128)S(1)} all-reduce(f32[64]{0:T(128)S(1)} %multiply_reduce_fusion.3), channel_id=1, replica_groups=mesh['dp'=8,'sy'=2,'sx'=2] {'dp','sy','sx'}, use_global_device_ids=true, to_apply=%region_55.56 | all-reduce | flops 64 | bytes 512 | tf_op jit(solution)/shard_map/psum | solution.py:64
  1088.1 38.9 %psum.177 = f32[256]{0:T(256)S(1)} all-reduce(f32[256]{0:T(256)S(1)} %get-tuple-element.158), channel_id=1, replica_groups=mesh['dp'=8,'sy'=2,'sx'=2] {'dp','sy','sx'}, use_global_device_ids=true, to_apply=%region_60.61 | all-reduce | flops 256 | bytes 2048 | tf_op jit(solution)/shard_map/psum | solution.py:62
  1127.2 41.2 %psum.178 = f32[256]{0:T(256)S(1)} all-reduce(f32[256]{0:T(256)S(1)} %multiply_reduce_fusion), channel_id=1, replica_groups=mesh['dp'=8,'sy'=2,'sx'=2] {'dp','sy','sx'}, use_global_device_ids=true, to_apply=%region_62.63 | all-reduce | flops 256 | bytes 2048 | tf_op jit(solution)/shard_map/psum | solution.py:64
  1169.3 6.0 psum.179
  1177.4 22.0 %psum.183 = f32[]{:T(128)} all-reduce(f32[]{:T(128)} %sub.104), channel_id=1, replica_groups=mesh['dp'=8,'sy'=2,'sx'=2] {'dp'}, use_global_device_ids=true, to_apply=%region_73.74 | all-reduce | flops 1 | bytes 8 | tf_op jit(solution)/shard_map/psum | solution.py:152
  (294 shorter events, 40.4 us)
Async XLA Ops:
  2.8 1.0 copy-start.17
  3.9 0.7 copy-start.22
  6.1 2.6 copy-start.20
  82.2 40.9 %copy-start.42 = (f32[3,2,64]{2,1,0:T(2,128)S(1)}, f32[3,2,64]{2,1,0:T(2,128)}, u32[]{:S(2)}) copy-start(f32[3,2,64]{2,1,0:T(2,128)} %param.26) | copy-start | bytes 4612
  82.4 40.7 %copy-start.41 = (f32[3,2,64]{2,1,0:T(2,128)S(1)}, f32[3,2,64]{2,1,0:T(2,128)}, u32[]{:S(2)}) copy-start(f32[3,2,64]{2,1,0:T(2,128)} %param.27) | copy-start | bytes 4612
  123.1 0.6 copy-start.51
  124.6 5.6 copy-start.9
  124.7 180.1 %collective-permute-start = (bf16[1,1,28,64]{3,2,1,0:T(8,128)(2,1)S(1)}, bf16[1,1,28,64]{3,2,1,0:T(8,128)(2,1)S(1)}, u32[]{:S(2)}, u32[]{:S(2)}) collective-permute-start(bf16[1,1,28,64]{3,2,1,0:T(8,128)(2,1)S(1)} %get-tuple-element.86), channel_id=1, source_target_pairs={{0,2},{1,3},{4,6},{5,7},{8,10},{9,11},{12,14},{13,15},{16,18},{17,... | collective-permute-start | bytes 10760 | tf_op jit(solution)/shard_map/ppermute | solution.py:20
  128.8 175.9 %collective-permute-start.1 = (bf16[1,1,28,64]{3,2,1,0:T(8,128)(2,1)S(1)}, bf16[1,1,28,64]{3,2,1,0:T(8,128)(2,1)S(1)}, u32[]{:S(2)}, u32[]{:S(2)}) collective-permute-start(bf16[1,1,28,64]{3,2,1,0:T(8,128)(2,1)S(1)} %get-tuple-element.85), channel_id=1, source_target_pairs={{2,0},{3,1},{6,4},{7,5},{10,8},{11,9},{14,12},{15,13},{18,16},{19,... | collective-permute-start | bytes 10760 | tf_op jit(solution)/shard_map/ppermute | solution.py:22
  130.6 32.7 %copy-start.18 = (bf16[2,3,64,32]{2,3,1,0:T(8,128)(2,1)S(1)}, bf16[2,3,64,32]{2,3,1,0:T(8,128)(2,1)}, u32[]{:S(2)}) copy-start(bf16[2,3,64,32]{2,3,1,0:T(8,128)(2,1)} %param.24) | copy-start | bytes 73732
  163.3 0.7 copy-start.21
  164.0 0.7 copy-start.43
  164.7 0.7 copy-start.44
  199.1 0.9 copy-start
  199.2 0.9 copy-start.16
  304.9 36.4 %collective-permute-start.2 = (bf16[1,30,1,64]{3,2,1,0:T(2,128)(2,1)S(1)}, bf16[1,30,1,64]{3,2,1,0:T(2,128)(2,1)S(1)}, u32[]{:S(2)}, u32[]{:S(2)}) collective-permute-start(bf16[1,30,1,64]{3,2,1,0:T(2,128)(2,1)S(1)} %get-tuple-element.71), channel_id=1, source_target_pairs={{0,1},{2,3},{4,5},{6,7},{8,9},{10,11},{12,13},{14,15},{16,17},{18,... | collective-permute-start | bytes 11528 | tf_op jit(solution)/shard_map/ppermute | solution.py:20
  306.2 35.1 %collective-permute-start.3 = (bf16[1,30,1,64]{3,2,1,0:T(2,128)(2,1)S(1)}, bf16[1,30,1,64]{3,2,1,0:T(2,128)(2,1)S(1)}, u32[]{:S(2)}, u32[]{:S(2)}) collective-permute-start(bf16[1,30,1,64]{3,2,1,0:T(2,128)(2,1)S(1)} %get-tuple-element.70), channel_id=1, source_target_pairs={{1,0},{3,2},{5,4},{7,6},{9,8},{11,10},{13,12},{15,14},{17,16},{19,... | collective-permute-start | bytes 11528 | tf_op jit(solution)/shard_map/ppermute | solution.py:22
  342.8 0.9 copy-start.3
  343.7 0.9 copy-start.6
  344.6 0.6 copy-start.34
  344.6 0.7 copy-start.52
  346.1 0.9 copy-start.1
  347.0 0.9 copy-start.11
  385.8 43.0 %copy-start.14 = (bf16[64,256]{0,1:T(8,128)(2,1)S(1)}, bf16[64,256]{0,1:T(8,128)(2,1)}, u32[]{:S(2)}) copy-start(bf16[64,256]{0,1:T(8,128)(2,1)} %all_gather.32) | copy-start | bytes 98308
  428.8 0.7 copy-start.49
  428.8 0.7 copy-start.50
  468.0 42.0 %copy-start.38 = (f32[1,256]{1,0:T(1,128)S(1)}, f32[1,256]{1,0:T(1,128)}, u32[]{:S(2)}) copy-start(f32[1,256]{1,0:T(1,128)} %get-tuple-element.108) | copy-start | bytes 3076
  510.0 0.7 copy-start.37
  510.7 0.8 copy-start.19
  592.1 0.6 copy-start.28
  592.1 0.6 copy-start.29
  593.0 4.3 copy-start.24
  593.1 38.0 %collective-permute-start.4 = (bf16[1,1,28,64]{3,2,1,0:T(8,128)(2,1)S(1)}, bf16[1,1,28,64]{3,2,1,0:T(8,128)(2,1)S(1)}, u32[]{:S(2)}, u32[]{:S(2)}) collective-permute-start(bf16[1,1,28,64]{3,2,1,0:T(8,128)(2,1)S(1)} %get-tuple-element.81), channel_id=1, source_target_pairs={{0,2},{1,3},{4,6},{5,7},{8,10},{9,11},{12,14},{13,15},{16,18},{17,... | collective-permute-start | bytes 10760 | tf_op jit(solution)/shard_map/ppermute | solution.py:20
  629.9 5.5 collective-permute-start.5
  635.6 34.3 %collective-permute-start.6 = (bf16[1,30,1,64]{3,2,1,0:T(2,128)(2,1)S(1)}, bf16[1,30,1,64]{3,2,1,0:T(2,128)(2,1)S(1)}, u32[]{:S(2)}, u32[]{:S(2)}) collective-permute-start(bf16[1,30,1,64]{3,2,1,0:T(2,128)(2,1)S(1)} %get-tuple-element.66), channel_id=1, source_target_pairs={{0,1},{2,3},{4,5},{6,7},{8,9},{10,11},{12,13},{14,15},{16,17},{18,... | collective-permute-start | bytes 11528 | tf_op jit(solution)/shard_map/ppermute | solution.py:20
  636.9 33.0 %collective-permute-start.7 = (bf16[1,30,1,64]{3,2,1,0:T(2,128)(2,1)S(1)}, bf16[1,30,1,64]{3,2,1,0:T(2,128)(2,1)S(1)}, u32[]{:S(2)}, u32[]{:S(2)}) collective-permute-start(bf16[1,30,1,64]{3,2,1,0:T(2,128)(2,1)S(1)} %get-tuple-element.65), channel_id=1, source_target_pairs={{1,0},{3,2},{5,4},{7,6},{9,8},{11,10},{13,12},{15,14},{17,16},{19,... | collective-permute-start | bytes 11528 | tf_op jit(solution)/shard_map/ppermute | solution.py:22
  674.5 0.9 copy-start.4
  675.4 0.9 copy-start.7
  676.3 0.6 copy-start.30
  676.3 0.7 copy-start.56
  677.8 0.9 copy-start.10
  716.0 41.2 %copy-start.13 = (bf16[64,256]{0,1:T(8,128)(2,1)S(1)}, bf16[64,256]{0,1:T(8,128)(2,1)}, u32[]{:S(2)}) copy-start(bf16[64,256]{0,1:T(8,128)(2,1)} %all_gather.35) | copy-start | bytes 98308
  757.2 0.6 copy-start.47
  757.2 0.6 copy-start.48
  798.0 40.4 %copy-start.36 = (f32[1,256]{1,0:T(1,128)S(1)}, f32[1,256]{1,0:T(1,128)}, u32[]{:S(2)}) copy-start(f32[1,256]{1,0:T(1,128)} %get-tuple-element.107) | copy-start | bytes 3076
  838.4 0.7 copy-start.35
  919.9 0.7 copy-start.25
  919.9 0.7 copy-start.26
  920.9 38.0 %collective-permute-start.8 = (bf16[1,1,28,64]{3,2,1,0:T(8,128)(2,1)S(1)}, bf16[1,1,28,64]{3,2,1,0:T(8,128)(2,1)S(1)}, u32[]{:S(2)}, u32[]{:S(2)}) collective-permute-start(bf16[1,1,28,64]{3,2,1,0:T(8,128)(2,1)S(1)} %get-tuple-element.76), channel_id=1, source_target_pairs={{0,2},{1,3},{4,6},{5,7},{8,10},{9,11},{12,14},{13,15},{16,18},{17,... | collective-permute-start | bytes 10760 | tf_op jit(solution)/shard_map/ppermute | solution.py:20
  957.6 5.5 collective-permute-start.9
  963.3 2.6 copy-start.23
  963.4 37.7 %collective-permute-start.10 = (bf16[1,30,1,64]{3,2,1,0:T(2,128)(2,1)S(1)}, bf16[1,30,1,64]{3,2,1,0:T(2,128)(2,1)S(1)}, u32[]{:S(2)}, u32[]{:S(2)}) collective-permute-start(bf16[1,30,1,64]{3,2,1,0:T(2,128)(2,1)S(1)} %get-tuple-element.61), channel_id=1, source_target_pairs={{0,1},{2,3},{4,5},{6,7},{8,9},{10,11},{12,13},{14,15},{16,17},{18,... | collective-permute-start | bytes 11528 | tf_op jit(solution)/shard_map/ppermute | solution.py:20
  964.7 36.4 %collective-permute-start.11 = (bf16[1,30,1,64]{3,2,1,0:T(2,128)(2,1)S(1)}, bf16[1,30,1,64]{3,2,1,0:T(2,128)(2,1)S(1)}, u32[]{:S(2)}, u32[]{:S(2)}) collective-permute-start(bf16[1,30,1,64]{3,2,1,0:T(2,128)(2,1)S(1)} %get-tuple-element.60), channel_id=1, source_target_pairs={{1,0},{3,2},{5,4},{7,6},{9,8},{11,10},{13,12},{15,14},{17,16},{19,... | collective-permute-start | bytes 11528 | tf_op jit(solution)/shard_map/ppermute | solution.py:22
  1002.6 0.9 copy-start.5
  1003.5 0.9 copy-start.8
  1004.4 0.6 copy-start.27
  1004.4 0.7 copy-start.54
  1005.9 0.9 copy-start.2
  1006.8 0.9 copy-start.12
  1045.0 42.0 %copy-start.15 = (bf16[64,256]{0,1:T(8,128)(2,1)S(1)}, bf16[64,256]{0,1:T(8,128)(2,1)}, u32[]{:S(2)}) copy-start(bf16[64,256]{0,1:T(8,128)(2,1)} %all_gather.38) | copy-start | bytes 98308
  1087.0 0.7 copy-start.45
  1087.0 0.7 copy-start.46
  1127.0 41.3 %copy-start.40 = (f32[1,256]{1,0:T(1,128)S(1)}, f32[1,256]{1,0:T(1,128)}, u32[]{:S(2)}) copy-start(f32[1,256]{1,0:T(1,128)} %get-tuple-element.109) | copy-start | bytes 3076
  1168.3 0.7 copy-start.39
  (5 other events, 2.6 us)
where the time goes:
time: 1210 us; the launch traced here: 1200 us
  blocking collectives  1100 us (91%)
  local copies, waits for them, and re-layouts  39.7 us (3%)
  starting transfers between devices  24.1 us (2%)
  other arithmetic  17.3 us (1%)
    psum x9, blocking collectives, normalize(): lax.psum(jnp.sum(centred * centred, axis=0), ('dp', 'sy', 'sx')) / count  372 us
    psum x9, blocking collectives, normalize(): mean = lax.psum(jnp.sum(y, axis=0), ('dp', 'sy', 'sx')) / count  345 us
    all_gather x9, blocking collectives, perturbed_product(): lax.all_gather(local, 'dp', axis=1, tiled=True)  291 us
    psum x1, blocking collectives, per_device(): lax.psum((jnp.sum(jnp.square(w_class.astype(jnp.float32)), axis=0), jnp.s...  36.1 us
    all_gather x1, blocking collectives, per_device(): lax.all_gather(local_class, 'dp', axis=0, tiled=True)  31.2 us
  transfers between devices with their start and end apart: 12, of which 2 were waited for; matrix products, arithmetic and copies ran while one was open for 1% of the time, Pallas kernels for 0%

commit v1 on v0

--- a/solution.py
+++ b/solution.py
@@ -61,7 +61,13 @@
 def normalize(y, gain, shift, count):
     mean = lax.psum(jnp.sum(y, axis=0), ("dp", "sy", "sx")) / count
     centred = y - mean
-    var = lax.psum(jnp.sum(centred * centred, axis=0), ("dp", "sy", "sx")) / count
+
+    def handle_the_layers_all(packet):
+        for dev_i in (("sy", "sx"), "dp"):
+            packet = lax.psum(packet, dev_i)
+        return packet
+
+    var = handle_the_layers_all(jnp.sum(centred * centred, axis=0)) / count
     return centred * lax.rsqrt(var + EPS_BN) * gain + shift
 
 

time: 1210 us -> 999 us (0.83)
  blocking collectives: 1100 us -> 924 us
  local copies, waits for them, and re-layouts: 39.7 us -> 11 us
    psum x10 -> x18, blocking collectives: 408 us -> 257 us  [handle_the_layers_all(): packet = lax.psum(packet, dev_i)]
    unnamed x138 -> x48, local copies, waits for them, and re-layouts: 21.2 us -> 1.55 us
    all_gather x9, blocking collectives: 291 us -> 277 us  [perturbed_product(): lax.all_gather(local, 'dp', axis=1, tiled=True)]
where the time goes in v1:
time: 999 us; the launch traced here: 996 us
  blocking collectives  924 us (92%)
  starting transfers between devices  25.2 us (3%)
  other arithmetic  17.5 us (2%)
  local copies, waits for them, and re-layouts  11 us (1%)
    psum x9, blocking collectives, normalize(): mean = lax.psum(jnp.sum(y, axis=0), ('dp', 'sy', 'sx')) / count  334 us
    all_gather x9, blocking collectives, perturbed_product(): lax.all_gather(local, 'dp', axis=1, tiled=True)  277 us
    psum x18, blocking collectives, handle_the_layers_all(): packet = lax.psum(packet, dev_i)  257 us
    all_gather x1, blocking collectives, per_device(): lax.all_gather(local_class, 'dp', axis=0, tiled=True)  31.4 us
  transfers between devices with their start and end apart: 12, of which 2 were waited for; matrix products, arithmetic and copies ran while one was open for 1% of the time, Pallas kernels for 0%

profile of v1, /device:TPU:0, one launch (start us, length us, event | category | flops | bytes accessed | tf_op | source)
XLA Modules:
  0.0 996.5 jit_solution(6861950664299770670)
XLA Ops:
  1.9 0.9 fusion.57
  2.8 0.9 multiply_reduce_fusion.11
  3.9 1.0 multiply_reduce_fusion.10
  4.9 1.3 multiply_multiply_fusion.5
  6.2 1.3 multiply_multiply_fusion.11
  7.5 1.3 multiply_multiply_fusion.17
  8.9 32.4 %all_gather.30 = bf16[256,64]{0,1:T(8,128)(2,1)S(1)} all-gather(bf16[256,8]{0,1:T(8,128)(2,1)S(1)} %get-tuple-element.101), channel_id=1, replica_groups=mesh['dp'=8,'sy'=2,'sx'=2] {'dp'}, dimensions={1}, use_global_device_ids=true | all-gather | bytes 36864 | tf_op jit(solution)/shard_map/all_gather | solution.py:57
  41.4 1.1 reshape.399
  42.8 39.6 %psum.224 = f32[64]{0:T(128)S(1)} all-reduce(f32[64]{0:T(128)S(1)} %get-tuple-element.143), channel_id=1, replica_groups=mesh['dp'=8,'sy'=2,'sx'=2] {'dp','sy','sx'}, use_global_device_ids=true, to_apply=%region_4.0 | all-reduce | flops 64 | bytes 512 | tf_op jit(solution)/shard_map/psum | solution.py:62
  82.6 5.8 psum.225
  88.4 20.4 %psum.226 = f32[64]{0:T(128)S(1)} all-reduce(f32[64]{0:T(128)S(1)} %psum.225), channel_id=1, replica_groups=mesh['dp'=8,'sy'=2,'sx'=2] {'dp'}, use_global_device_ids=true, to_apply=%region_7.0 | all-reduce | flops 64 | bytes 512 | tf_op jit(solution)/shard_map/psum | solution.py:67
  109.3 1.4 collective-permute-start.1
  110.7 4.5 collective-permute-start
  118.1 30.5 %all_gather.31 = bf16[576,64]{0,1:T(8,128)(2,1)S(1)} all-gather(bf16[576,8]{0,1:T(8,128)(2,1)S(1)} %add_convert_fusion.2), channel_id=1, replica_groups=mesh['dp'=8,'sy'=2,'sx'=2] {'dp'}, dimensions={1}, use_global_device_ids=true | all-gather | bytes 82944 | tf_op jit(solution)/shard_map/all_gather | solution.py:57
  148.7 30.5 %all_gather.34 = bf16[576,64]{0,1:T(8,128)(2,1)S(1)} all-gather(bf16[576,8]{0,1:T(8,128)(2,1)S(1)} %add_convert_fusion.1), channel_id=1, replica_groups=mesh['dp'=8,'sy'=2,'sx'=2] {'dp'}, dimensions={1}, use_global_device_ids=true | all-gather | bytes 82944 | tf_op jit(solution)/shard_map/all_gather | solution.py:57
  179.2 1.3 multiply_multiply_fusion.15
  180.6 1.3 multiply_multiply_fusion.3
  182.0 30.6 %all_gather.33 = bf16[256,64]{0,1:T(8,128)(2,1)S(1)} all-gather(bf16[256,8]{0,1:T(8,128)(2,1)S(1)} %get-tuple-element.102), channel_id=1, replica_groups=mesh['dp'=8,'sy'=2,'sx'=2] {'dp'}, dimensions={1}, use_global_device_ids=true | all-gather | bytes 36864 | tf_op jit(solution)/shard_map/all_gather | solution.py:57
  212.8 1.3 collective-permute-start.3
  214.1 3.0 collective-permute-start.2
  217.1 30.5 %all_gather.32 = bf16[64,256]{0,1:T(8,128)(2,1)S(1)} all-gather(bf16[64,32]{0,1:T(8,128)(2,1)S(1)} %get-tuple-element.96), channel_id=1, replica_groups=mesh['dp'=8,'sy'=2,'sx'=2] {'dp'}, dimensions={1}, use_global_device_ids=true | all-gather | bytes 36864 | tf_op jit(solution)/shard_map/all_gather | solution.py:57
  250.6 36.8 %psum.227 = f32[64]{0:T(128)S(1)} all-reduce(f32[64]{0:T(128)S(1)} %get-tuple-element.145), channel_id=1, replica_groups=mesh['dp'=8,'sy'=2,'sx'=2] {'dp','sy','sx'}, use_global_device_ids=true, to_apply=%region_12.13 | all-reduce | flops 64 | bytes 512 | tf_op jit(solution)/shard_map/psum | solution.py:62
  287.6 5.8 psum.228
  293.4 21.0 %psum.229 = f32[64]{0:T(128)S(1)} all-reduce(f32[64]{0:T(128)S(1)} %psum.228), channel_id=1, replica_groups=mesh['dp'=8,'sy'=2,'sx'=2] {'dp'}, use_global_device_ids=true, to_apply=%region_15.16 | all-reduce | flops 64 | bytes 512 | tf_op jit(solution)/shard_map/psum | solution.py:67
  314.9 36.8 %psum.230 = f32[256]{0:T(256)S(1)} all-reduce(f32[256]{0:T(256)S(1)} %get-tuple-element.147), channel_id=1, replica_groups=mesh['dp'=8,'sy'=2,'sx'=2] {'dp','sy','sx'}, use_global_device_ids=true, to_apply=%region_20.21 | all-reduce | flops 256 | bytes 2048 | tf_op jit(solution)/shard_map/psum | solution.py:62
  351.9 5.8 psum.231
  357.8 21.0 %psum.232 = f32[256]{0:T(256)S(1)} all-reduce(f32[256]{0:T(256)S(1)} %psum.231), channel_id=1, replica_groups=mesh['dp'=8,'sy'=2,'sx'=2] {'dp'}, use_global_device_ids=true, to_apply=%region_23.24 | all-reduce | flops 256 | bytes 2048 | tf_op jit(solution)/shard_map/psum | solution.py:67
  379.4 36.8 %psum.233 = f32[64]{0:T(128)S(1)} all-reduce(f32[64]{0:T(128)S(1)} %get-tuple-element.149), channel_id=1, replica_groups=mesh['dp'=8,'sy'=2,'sx'=2] {'dp','sy','sx'}, use_global_device_ids=true, to_apply=%region_28.29 | all-reduce | flops 64 | bytes 512 | tf_op jit(solution)/shard_map/psum | solution.py:62
  416.4 5.8 psum.234
  422.3 21.0 %psum.235 = f32[64]{0:T(128)S(1)} all-reduce(f32[64]{0:T(128)S(1)} %psum.234), channel_id=1, replica_groups=mesh['dp'=8,'sy'=2,'sx'=2] {'dp'}, use_global_device_ids=true, to_apply=%region_31.32 | all-reduce | flops 64 | bytes 512 | tf_op jit(solution)/shard_map/psum | solution.py:67
  443.7 1.8 collective-permute-start.4
  445.6 30.6 %all_gather.36 = bf16[256,64]{0,1:T(8,128)(2,1)S(1)} all-gather(bf16[256,8]{0,1:T(8,128)(2,1)S(1)} %get-tuple-element.100), channel_id=1, replica_groups=mesh['dp'=8,'sy'=2,'sx'=2] {'dp'}, dimensions={1}, use_global_device_ids=true | all-gather | bytes 36864 | tf_op jit(solution)/shard_map/all_gather | solution.py:57
  476.2 1.3 collective-permute-start.5
  477.5 4.2 collective-permute-done.5
  481.9 1.3 collective-permute-start.7
  483.2 3.0 collective-permute-start.6
  486.2 30.7 %all_gather.35 = bf16[64,256]{0,1:T(8,128)(2,1)S(1)} all-gather(bf16[64,32]{0,1:T(8,128)(2,1)S(1)} %get-tuple-element.94), channel_id=1, replica_groups=mesh['dp'=8,'sy'=2,'sx'=2] {'dp'}, dimensions={1}, use_global_device_ids=true | all-gather | bytes 36864 | tf_op jit(solution)/shard_map/all_gather | solution.py:57
  519.8 36.8 %psum.236 = f32[64]{0:T(128)S(1)} all-reduce(f32[64]{0:T(128)S(1)} %get-tuple-element.151), channel_id=1, replica_groups=mesh['dp'=8,'sy'=2,'sx'=2] {'dp','sy','sx'}, use_global_device_ids=true, to_apply=%region_36.37 | all-reduce | flops 64 | bytes 512 | tf_op jit(solution)/shard_map/psum | solution.py:62
  556.8 5.8 psum.237
  562.7 21.0 %psum.238 = f32[64]{0:T(128)S(1)} all-reduce(f32[64]{0:T(128)S(1)} %psum.237), channel_id=1, replica_groups=mesh['dp'=8,'sy'=2,'sx'=2] {'dp'}, use_global_device_ids=true, to_apply=%region_39.40 | all-reduce | flops 64 | bytes 512 | tf_op jit(solution)/shard_map/psum | solution.py:67
  584.2 36.8 %psum.239 = f32[256]{0:T(256)S(1)} all-reduce(f32[256]{0:T(256)S(1)} %get-tuple-element.153), channel_id=1, replica_groups=mesh['dp'=8,'sy'=2,'sx'=2] {'dp','sy','sx'}, use_global_device_ids=true, to_apply=%region_44.45 | all-reduce | flops 256 | bytes 2048 | tf_op jit(solution)/shard_map/psum | solution.py:62
  621.2 5.8 psum.240
  627.0 21.0 %psum.241 = f32[256]{0:T(256)S(1)} all-reduce(f32[256]{0:T(256)S(1)} %psum.240), channel_id=1, replica_groups=mesh['dp'=8,'sy'=2,'sx'=2] {'dp'}, use_global_device_ids=true, to_apply=%region_47.48 | all-reduce | flops 256 | bytes 2048 | tf_op jit(solution)/shard_map/psum | solution.py:67
  648.6 36.8 %psum.242 = f32[64]{0:T(128)S(1)} all-reduce(f32[64]{0:T(128)S(1)} %get-tuple-element.155), channel_id=1, replica_groups=mesh['dp'=8,'sy'=2,'sx'=2] {'dp','sy','sx'}, use_global_device_ids=true, to_apply=%region_52.53 | all-reduce | flops 64 | bytes 512 | tf_op jit(solution)/shard_map/psum | solution.py:62
  685.7 5.8 psum.243
  691.5 21.0 %psum.244 = f32[64]{0:T(128)S(1)} all-reduce(f32[64]{0:T(128)S(1)} %psum.243), channel_id=1, replica_groups=mesh['dp'=8,'sy'=2,'sx'=2] {'dp'}, use_global_device_ids=true, to_apply=%region_55.56 | all-reduce | flops 64 | bytes 512 | tf_op jit(solution)/shard_map/psum | solution.py:67
  713.0 1.8 collective-permute-start.8
  714.8 30.5 %all_gather.37 = bf16[576,64]{0,1:T(8,128)(2,1)S(1)} all-gather(bf16[576,8]{0,1:T(8,128)(2,1)S(1)} %add_convert_fusion), channel_id=1, replica_groups=mesh['dp'=8,'sy'=2,'sx'=2] {'dp'}, dimensions={1}, use_global_device_ids=true | all-gather | bytes 82944 | tf_op jit(solution)/shard_map/all_gather | solution.py:57
  745.4 1.3 collective-permute-start.9
  746.7 4.2 collective-permute-done.9
  751.0 1.3 collective-permute-start.11
  752.4 3.0 collective-permute-start.10
  755.4 30.5 %all_gather.38 = bf16[64,256]{0,1:T(8,128)(2,1)S(1)} all-gather(bf16[64,32]{0,1:T(8,128)(2,1)S(1)} %get-tuple-element.95), channel_id=1, replica_groups=mesh['dp'=8,'sy'=2,'sx'=2] {'dp'}, dimensions={1}, use_global_device_ids=true | all-gather | bytes 36864 | tf_op jit(solution)/shard_map/all_gather | solution.py:57
  789.5 36.8 %psum.245 = f32[64]{0:T(128)S(1)} all-reduce(f32[64]{0:T(128)S(1)} %get-tuple-element.157), channel_id=1, replica_groups=mesh['dp'=8,'sy'=2,'sx'=2] {'dp','sy','sx'}, use_global_device_ids=true, to_apply=%region_60.61 | all-reduce | flops 64 | bytes 512 | tf_op jit(solution)/shard_map/psum | solution.py:62
  826.5 5.8 psum.246
  832.3 21.0 %psum.247 = f32[64]{0:T(128)S(1)} all-reduce(f32[64]{0:T(128)S(1)} %psum.246), channel_id=1, replica_groups=mesh['dp'=8,'sy'=2,'sx'=2] {'dp'}, use_global_device_ids=true, to_apply=%region_63.64 | all-reduce | flops 64 | bytes 512 | tf_op jit(solution)/shard_map/psum | solution.py:67
  853.8 36.8 %psum.248 = f32[256]{0:T(256)S(1)} all-reduce(f32[256]{0:T(256)S(1)} %get-tuple-element.159), channel_id=1, replica_groups=mesh['dp'=8,'sy'=2,'sx'=2] {'dp','sy','sx'}, use_global_device_ids=true, to_apply=%region_68.69 | all-reduce | flops 256 | bytes 2048 | tf_op jit(solution)/shard_map/psum | solution.py:62
  890.8 5.8 psum.249
  896.7 36.7 %all-reduce = (f32[256]{0:T(256)S(1)}, f32[1000]{0:T(1024)S(1)}, f32[1000]{0:T(1024)S(1)}, f32[1000]{0:T(1024)S(1)}) all-reduce(f32[256]{0:T(256)S(1)} %psum.249, f32[1000]{0:T(1024)S(1)} %get-tuple-element.4, f32[1000]{0:T(1024)S(1)} %fusion.12, f32[1000]{0:T(1024)S(1)} %get-tuple-element.3), channel_id=1, replica_groups=mesh['dp'=8,'sy'=2,'sx'=2] {'dp'}, use_global_device_ids=true, to_apply=%region_71.72 | all-reduce | flops 3256 | bytes 26048 | tf_op jit(solution)/shard_map/psum | solution.py:67
  933.7 5.8 psum.251
  939.4 1.3 multiply_multiply_fusion.1
  940.8 31.4 %all_gather.39 = bf16[256,1000]{1,0:T(8,128)(2,1)S(1)} all-gather(bf16[32,1000]{1,0:T(8,128)(2,1)S(1)} %fusion.14), channel_id=1, replica_groups=mesh['dp'=8,'sy'=2,'sx'=2] {'dp'}, dimensions={0}, use_global_device_ids=true | all-gather | bytes 576000 | tf_op jit(solution)/shard_map/all_gather | solution.py:151
  974.3 18.4 %psum.255 = f32[]{:T(128)} all-reduce(f32[]{:T(128)} %sub.104), channel_id=1, replica_groups=mesh['dp'=8,'sy'=2,'sx'=2] {'dp'}, use_global_device_ids=true, to_apply=%region_82.83 | all-reduce | flops 1 | bytes 8 | tf_op jit(solution)/shard_map/psum | solution.py:158
  992.7 0.8 reshape.403
  (213 shorter events, 19.9 us)
Async XLA Ops:
  2.7 0.9 copy-start.5
  7.5 1.3 copy-start.7
  82.4 26.5 %copy-start.9 = (f32[3,2,64]{2,1,0:T(2,128)S(1)}, f32[3,2,64]{2,1,0:T(2,128)}, u32[]{:S(2)}) copy-start(f32[3,2,64]{2,1,0:T(2,128)} %param.26) | copy-start | bytes 4612
  82.6 26.3 %copy-start.8 = (f32[3,2,64]{2,1,0:T(2,128)S(1)}, f32[3,2,64]{2,1,0:T(2,128)}, u32[]{:S(2)}) copy-start(f32[3,2,64]{2,1,0:T(2,128)} %param.27) | copy-start | bytes 4612
  109.2 6.1 copy-start.3
  109.3 6.0 copy-start.1
  109.3 103.3 %collective-permute-start.1 = (bf16[1,1,28,64]{3,2,1,0:T(8,128)(2,1)S(1)}, bf16[1,1,28,64]{3,2,1,0:T(8,128)(2,1)S(1)}, u32[]{:S(2)}, u32[]{:S(2)}) collective-permute-start(bf16[1,1,28,64]{3,2,1,0:T(8,128)(2,1)S(1)} %get-tuple-element.86), channel_id=1, source_target_pairs={{2,0},{3,1},{6,4},{7,5},{10,8},{11,9},{14,12},{15,13},{18,16},{19,... | collective-permute-start | bytes 10760 | tf_op jit(solution)/shard_map/ppermute | solution.py:22
  110.7 101.9 %collective-permute-start = (bf16[1,1,28,64]{3,2,1,0:T(8,128)(2,1)S(1)}, bf16[1,1,28,64]{3,2,1,0:T(8,128)(2,1)S(1)}, u32[]{:S(2)}, u32[]{:S(2)}) collective-permute-start(bf16[1,1,28,64]{3,2,1,0:T(8,128)(2,1)S(1)} %get-tuple-element.87), channel_id=1, source_target_pairs={{0,2},{1,3},{4,6},{5,7},{8,10},{9,11},{12,14},{13,15},{16,18},{17,... | collective-permute-start | bytes 10760 | tf_op jit(solution)/shard_map/ppermute | solution.py:20
  115.3 0.7 copy-start.6
  115.3 0.9 copy-start.4
  115.3 1.1 copy-start.10
  115.3 1.1 copy-start.11
  115.4 1.1 copy-start.2
  116.1 0.9 copy-start
  212.8 35.3 %collective-permute-start.3 = (bf16[1,30,1,64]{3,2,1,0:T(2,128)(2,1)S(1)}, bf16[1,30,1,64]{3,2,1,0:T(2,128)(2,1)S(1)}, u32[]{:S(2)}, u32[]{:S(2)}) collective-permute-start(bf16[1,30,1,64]{3,2,1,0:T(2,128)(2,1)S(1)} %get-tuple-element.71), channel_id=1, source_target_pairs={{1,0},{3,2},{5,4},{7,6},{9,8},{11,10},{13,12},{15,14},{17,16},{19,... | collective-permute-start | bytes 11528 | tf_op jit(solution)/shard_map/ppermute | solution.py:22
  214.1 34.0 %collective-permute-start.2 = (bf16[1,30,1,64]{3,2,1,0:T(2,128)(2,1)S(1)}, bf16[1,30,1,64]{3,2,1,0:T(2,128)(2,1)S(1)}, u32[]{:S(2)}, u32[]{:S(2)}) collective-permute-start(bf16[1,30,1,64]{3,2,1,0:T(2,128)(2,1)S(1)} %get-tuple-element.72), channel_id=1, source_target_pairs={{0,1},{2,3},{4,5},{6,7},{8,9},{10,11},{12,13},{14,15},{16,17},{18,... | collective-permute-start | bytes 11528 | tf_op jit(solution)/shard_map/ppermute | solution.py:20
  443.7 33.8 %collective-permute-start.4 = (bf16[1,1,28,64]{3,2,1,0:T(8,128)(2,1)S(1)}, bf16[1,1,28,64]{3,2,1,0:T(8,128)(2,1)S(1)}, u32[]{:S(2)}, u32[]{:S(2)}) collective-permute-start(bf16[1,1,28,64]{3,2,1,0:T(8,128)(2,1)S(1)} %get-tuple-element.82), channel_id=1, source_target_pairs={{0,2},{1,3},{4,6},{5,7},{8,10},{9,11},{12,14},{13,15},{16,18},{17,... | collective-permute-start | bytes 10760 | tf_op jit(solution)/shard_map/ppermute | solution.py:20
  476.2 5.5 collective-permute-start.5
  481.9 35.5 %collective-permute-start.7 = (bf16[1,30,1,64]{3,2,1,0:T(2,128)(2,1)S(1)}, bf16[1,30,1,64]{3,2,1,0:T(2,128)(2,1)S(1)}, u32[]{:S(2)}, u32[]{:S(2)}) collective-permute-start(bf16[1,30,1,64]{3,2,1,0:T(2,128)(2,1)S(1)} %get-tuple-element.66), channel_id=1, source_target_pairs={{1,0},{3,2},{5,4},{7,6},{9,8},{11,10},{13,12},{15,14},{17,16},{19,... | collective-permute-start | bytes 11528 | tf_op jit(solution)/shard_map/ppermute | solution.py:22
  483.2 34.2 %collective-permute-start.6 = (bf16[1,30,1,64]{3,2,1,0:T(2,128)(2,1)S(1)}, bf16[1,30,1,64]{3,2,1,0:T(2,128)(2,1)S(1)}, u32[]{:S(2)}, u32[]{:S(2)}) collective-permute-start(bf16[1,30,1,64]{3,2,1,0:T(2,128)(2,1)S(1)} %get-tuple-element.67), channel_id=1, source_target_pairs={{0,1},{2,3},{4,5},{6,7},{8,9},{10,11},{12,13},{14,15},{16,17},{18,... | collective-permute-start | bytes 11528 | tf_op jit(solution)/shard_map/ppermute | solution.py:20
  713.0 33.7 %collective-permute-start.8 = (bf16[1,1,28,64]{3,2,1,0:T(8,128)(2,1)S(1)}, bf16[1,1,28,64]{3,2,1,0:T(8,128)(2,1)S(1)}, u32[]{:S(2)}, u32[]{:S(2)}) collective-permute-start(bf16[1,1,28,64]{3,2,1,0:T(8,128)(2,1)S(1)} %get-tuple-element.77), channel_id=1, source_target_pairs={{0,2},{1,3},{4,6},{5,7},{8,10},{9,11},{12,14},{13,15},{16,18},{17,... | collective-permute-start | bytes 10760 | tf_op jit(solution)/shard_map/ppermute | solution.py:20
  745.4 5.5 collective-permute-start.9
  751.0 36.0 %collective-permute-start.11 = (bf16[1,30,1,64]{3,2,1,0:T(2,128)(2,1)S(1)}, bf16[1,30,1,64]{3,2,1,0:T(2,128)(2,1)S(1)}, u32[]{:S(2)}, u32[]{:S(2)}) collective-permute-start(bf16[1,30,1,64]{3,2,1,0:T(2,128)(2,1)S(1)} %get-tuple-element.61), channel_id=1, source_target_pairs={{1,0},{3,2},{5,4},{7,6},{9,8},{11,10},{13,12},{15,14},{17,16},{19,... | collective-permute-start | bytes 11528 | tf_op jit(solution)/shard_map/ppermute | solution.py:22
  752.4 34.7 %collective-permute-start.10 = (bf16[1,30,1,64]{3,2,1,0:T(2,128)(2,1)S(1)}, bf16[1,30,1,64]{3,2,1,0:T(2,128)(2,1)S(1)}, u32[]{:S(2)}, u32[]{:S(2)}) collective-permute-start(bf16[1,30,1,64]{3,2,1,0:T(2,128)(2,1)S(1)} %get-tuple-element.62), channel_id=1, source_target_pairs={{0,1},{2,3},{4,5},{6,7},{8,9},{10,11},{12,13},{14,15},{16,17},{18,... | collective-permute-start | bytes 11528 | tf_op jit(solution)/shard_map/ppermute | solution.py:20
